TPU v7x, 256 devices: a whole 4x4x8 slice. The times are simulated.
256 devices in a mesh: sub: 4 (over x), row: 4 (over y_lo, core), col: 16 (over z, y_hi).
Axes of the slice: x: 4, y: 4 (y_hi: 2, y_lo: 2; y = y_hi * 2 + y_lo), z: 8, core: 2. Of those that a mesh axis runs over, the one named last changes fastest.
Arguments:
- leaf_sizes: int32 [512], P(('sub', 'row', 'col')), may hold values from 20 to 219
- remap: int32 [4], replicated, may hold values from 0 to 3, each once
- panel_diag: float32 [4, 1536, 1536], P('sub', ('row', 'col')), may hold values from -1 to 6, as said below
- panel_below: float32 [4, 5632, 1536], P('sub', ('row', 'col')), may hold values from -1.2 to 1.2
- trailing: float32 [4, 5632, 5632], P('sub', 'row', 'col'), may hold values from -6 to 26, as said below
Outputs:
- diag_factor: float32 [4, 1536, 1536], P('sub', ('row', 'col'))
- panel_factor: float32 [4, 5632, 1536], P('sub', ('row', 'col'))
- schur: float32 [4, 5632, 5632], P('sub', 'row', 'col')
- subtree_cost: float32 [4], P('sub')
Inputs may be any that keep to these rules, and one draw needn't show every extreme that they name: remap is a permutation: front j moves to subcube remap[j]. `panel_diag`: each front's block is symmetric and positive definite. `trailing`: each front's block is symmetric.
All inputs are finite; a program needn't handle non-finite values.
Results may differ from a plain program's by a relative error of at most 0.0001.
Values sent between devices are 32-bit elements; how exact they have to be, the bound alone decides.
No kernel may reach another device: no remote copies, remote signals or barrier semaphores. Data moves between devices by JAX's collectives and lax.ppermute only.
A program may use at most 128 MiB of HBM per device.

v0:
```python
import jax
import jax.numpy as jnp
from jax import lax
from jax.sharding import Mesh
from jax.sharding import PartitionSpec as P

ROW = ("row_0", "row_1")
COL = ("col_0", "col_1")
ROW_COL = ("row_0", "row_1", "col_0", "col_1")
SUB_ROW_COL = ("sub", "row_0", "row_1", "col_0", "col_1")


def from_everyone(value, axis):
    copies = jnp.broadcast_to(value, (lax.axis_size(axis), *value.shape))
    return lax.all_to_all(copies, axis, split_axis=0, concat_axis=0, tiled=True)


def taken_together(value, axis):
    everything = from_everyone(value, axis)
    return jnp.sum(everything, axis=0)


def in_one_piece(arrays, axis, split_dim, concat_dim, along):
    ends, at = ([], 0)
    for a in arrays[:-1]:
        at += a.shape[along]
        ends.append(at)
    both = jnp.concatenate(arrays, axis=along)
    return tuple(
        jnp.split(
            lax.all_to_all(both, axis, split_axis=split_dim, concat_axis=concat_dim, tiled=True),
            ends,
            axis=along,
        )
    )


def joined_along(pieces, dim):
    shape = list(pieces.shape[1:])
    shape[dim] *= pieces.shape[0]
    return jnp.moveaxis(pieces, 0, dim).reshape(shape)


def gather_in_order(value, axes, order):
    pieces = value[None]
    for k in order:
        pieces = lax.all_gather(pieces, axes[k], axis=0, tiled=True)
    block = [lax.axis_size(axes[k]) for k in reversed(order)]
    pieces = pieces.reshape(*block, *value.shape)
    turned = sorted(range(len(order)), key=lambda place: order[len(order) - 1 - place])
    return pieces.transpose(*turned, *range(len(order), pieces.ndim)).reshape(-1, *value.shape)


def gather_axes(value, axes, order, dim):
    return joined_along(gather_in_order(value, axes, order), dim)


def broadcast(value, axis, root):
    return lax.dynamic_index_in_dim(lax.all_gather(value, axis), root, 0, keepdims=False)


def column_rows(row_block, rows_count, cols_count, column, sender):
    block_rows = row_block.shape[0]
    col_rows = block_rows * rows_count // cols_count
    per_part = min(col_rows, block_rows)
    begin_row = column * col_rows + 0
    holder = begin_row // block_rows
    offset = begin_row % block_rows
    pieces = sender(lax.dynamic_slice_in_dim(row_block, offset, per_part, 0), holder)
    return pieces


def local(leaf_sizes, remap, panel_diag, panel_below, trailing):
    rows_count = lax.axis_size(ROW)
    cols_count = lax.axis_size(COL)
    scaled = leaf_sizes.astype(jnp.float32) / 100.0
    partial_cost = jnp.sum(scaled * scaled * scaled)
    summed = taken_together(partial_cost, ROW_COL)
    subtree_cost = jnp.reshape(summed / (leaf_sizes.shape[0] * rows_count * cols_count), (1,))
    front_count = remap.shape[0]
    counter = jnp.arange(front_count, dtype=jnp.int32)
    sources = jnp.sum(
        counter[None, :] * (remap[None, :] == counter[:, None]).astype(jnp.int32), axis=1
    )
    spread = (
        *in_one_piece((panel_diag, panel_below), "sub", 2, 0, 1),
        lax.all_to_all(trailing, "sub", split_axis=2, concat_axis=0, tiled=True),
    )
    ordered = (
        jnp.take(spread[0], sources, axis=0),
        jnp.take(spread[1], sources, axis=0),
        jnp.take(spread[2], sources, axis=0),
    )
    mine = (
        *in_one_piece((ordered[0], ordered[1]), "sub", 0, 2, 1),
        lax.all_to_all(ordered[2], "sub", split_axis=0, concat_axis=2, tiled=True),
    )
    diag_block = mine[0][0]
    below_block = mine[1][0]
    trail_block = mine[2][0]
    gathered = gather_axes(diag_block, ROW_COL, (3, 0, 2, 1), 0)
    factor_low = jnp.linalg.cholesky(gathered)
    column = lax.axis_index(COL)
    flat_index = lax.axis_index(ROW) * cols_count + column
    diag_count = diag_block.shape[0]
    diag_factor = lax.dynamic_slice_in_dim(factor_low, flat_index * diag_count, diag_count, 0)
    own_rows = lax.linalg.triangular_solve(
        factor_low, below_block, left_side=False, lower=True, transpose_a=True
    )
    row_block = lax.all_gather(own_rows, COL, axis=0, tiled=True)
    col_block = column_rows(
        row_block,
        rows_count,
        cols_count,
        column,
        lambda block_part, root_index: broadcast(block_part, ROW, root_index),
    )
    update = lax.dot_general(
        row_block,
        col_block,
        (((1,), (1,)), ((), ())),
        precision=lax.Precision.HIGHEST,
        preferred_element_type=jnp.float32,
    )
    schur_block = trail_block - update
    return (diag_factor[None], own_rows[None], schur_block[None], subtree_cost)


def solution(mesh):
    finer = Mesh(
        mesh.devices.reshape(mesh.shape["sub"], 2, 2, 8, 2),
        ("sub", "row_0", "row_1", "col_0", "col_1"),
    )
    return jax.shard_map(
        local,
        mesh=finer,
        in_specs=(
            P(SUB_ROW_COL),
            P(),
            P("sub", ROW_COL, None),
            P("sub", ROW_COL, None),
            P("sub", ROW, COL),
        ),
        out_specs=(P("sub", ROW_COL, None), P("sub", ROW_COL, None), P("sub", ROW, COL), P("sub")),
        check_vma=False,
    )
```

profile of v0, /device:TPU:1, one launch (start us, length us, event | category | flops | bytes accessed | tf_op | source)
XLA Modules:
  0.0 948.4 jit_solution(2037040901221429000)
XLA Ops:
  26.8 10.4 %all_to_all.75 = f32[4,112,384]{2,1,0:T(8,128)S(1)} all-to-all(f32[4,112,384]{2,1,0:T(8,128)S(1)} %pad_maximum_fusion.1), channel_id=1, replica_groups=mesh['sub'=4,'row_0'=2,'row_1'=2,'col_0'=8,'col_1'=2] {'sub'}, dimensions={0} | all-to-all | bytes 1376256 | tf_op jit(solution)/shard_map/all_to_all | solution.py:31
  53.0 64.9 %all-gather.6.cloned.1.call-done = f32[32,24,1536]{2,1,0:T(8,128)} async-done(((f32[4,24,1536]{2,1,0:T(8,128)}), f32[32,24,1536]{2,1,0:T(8,128)}) %all-gather.6.cloned.1.call-update) | async-done | bytes 4718608 | tf_op jit(solution)/shard_map/all_gather | solution.py:47
  118.0 28.2 %all-gather.8.cloned.1.call-done = f32[64,24,1536]{2,1,0:T(8,128)} async-done(((f32[32,24,1536]{2,1,0:T(8,128)}), f32[64,24,1536]{2,1,0:T(8,128)}) %all-gather.8.cloned.1.call-update) | async-done | bytes 9437200 | tf_op jit(solution)/shard_map/all_gather | solution.py:47
  155.0 10.1 %copy.43 = f32[1536,1536]{0,1:T(8,128)} copy(f32[1536,1536]{1,0:T(8,128)} %bitcast.191) | data formatting | bytes 18874368 | tf_op jit(solution)/shard_map/reshape;reshape | solution.py:41
  165.1 12.3 %fusion = f32[1536,1536]{1,0:T(8,128)} fusion(f32[1536,1536]{0,1:T(8,128)} %copy.43, f32[2,2,8,2,24,1536]{5,4,3,2,1,0:T(8,128)} %copy.42), kind=kLoop, calls=%fused_computation.6 | loop fusion | flops 4718592 | bytes 28311552 | tf_op jit(solution)/shard_map/jit(cholesky)/div | solution.py:102
  178.2 11.7 %cholesky.341 = f32[128,128]{1,0:T(8,128)S(1)} custom-call(f32[128,128]{1,0:T(8,128)S(1)} %cholesky.892), custom_call_target="Cholesky" | custom-call | tf_op jit(solution)/shard_map/jit(cholesky)/cholesky | solution.py:102
  209.4 11.9 %cholesky.362 = f32[128,128]{1,0:T(8,128)S(1)} custom-call(f32[128,128]{1,0:T(8,128)S(1)} %cholesky.896), custom_call_target="Cholesky" | custom-call | tf_op jit(solution)/shard_map/jit(cholesky)/cholesky | solution.py:102
  236.1 11.7 %cholesky.385 = f32[128,128]{1,0:T(8,128)S(1)} custom-call(f32[128,128]{1,0:T(8,128)S(1)} %cholesky.901), custom_call_target="Cholesky" | custom-call | tf_op jit(solution)/shard_map/jit(cholesky)/cholesky | solution.py:102
  263.3 11.7 %cholesky.715 = f32[128,128]{1,0:T(8,128)S(1)} custom-call(f32[128,128]{1,0:T(8,128)S(1)} %cholesky.906), custom_call_target="Cholesky" | custom-call | tf_op jit(solution)/shard_map/jit(cholesky)/cholesky | solution.py:102
  290.6 12.1 %cholesky.734 = f32[128,128]{1,0:T(8,128)S(1)} custom-call(f32[128,128]{1,0:T(8,128)S(1)} %cholesky.911), custom_call_target="Cholesky" | custom-call | tf_op jit(solution)/shard_map/jit(cholesky)/cholesky | solution.py:102
  318.4 11.7 %cholesky.754 = f32[128,128]{1,0:T(8,128)S(1)} custom-call(f32[128,128]{1,0:T(8,128)S(1)} %cholesky.916), custom_call_target="Cholesky" | custom-call | tf_op jit(solution)/shard_map/jit(cholesky)/cholesky | solution.py:102
  345.8 11.7 %cholesky.774 = f32[128,128]{1,0:T(8,128)S(1)} custom-call(f32[128,128]{1,0:T(8,128)S(1)} %cholesky.921), custom_call_target="Cholesky" | custom-call | tf_op jit(solution)/shard_map/jit(cholesky)/cholesky | solution.py:102
  373.2 11.7 %cholesky.794 = f32[128,128]{1,0:T(8,128)S(1)} custom-call(f32[128,128]{1,0:T(8,128)S(1)} %cholesky.926), custom_call_target="Cholesky" | custom-call | tf_op jit(solution)/shard_map/jit(cholesky)/cholesky | solution.py:102
  400.1 12.1 %cholesky.814 = f32[128,128]{1,0:T(8,128)S(1)} custom-call(f32[128,128]{1,0:T(8,128)S(1)} %cholesky.931), custom_call_target="Cholesky" | custom-call | tf_op jit(solution)/shard_map/jit(cholesky)/cholesky | solution.py:102
  426.9 11.7 %cholesky.834 = f32[128,128]{1,0:T(8,128)S(1)} custom-call(f32[128,128]{1,0:T(8,128)S(1)} %cholesky.936), custom_call_target="Cholesky" | custom-call | tf_op jit(solution)/shard_map/jit(cholesky)/cholesky | solution.py:102
  452.8 11.9 %cholesky.854 = f32[128,128]{1,0:T(8,128)S(1)} custom-call(f32[128,128]{1,0:T(8,128)S(1)} %cholesky.941), custom_call_target="Cholesky" | custom-call | tf_op jit(solution)/shard_map/jit(cholesky)/cholesky | solution.py:102
  478.2 11.7 %cholesky.872 = f32[128,128]{1,0:T(8,128)S(1)} custom-call(f32[128,128]{1,0:T(8,128)S(1)} %convolution_subtract_fusion.4), custom_call_target="Cholesky" | custom-call | tf_op jit(solution)/shard_map/jit(cholesky)/cholesky | solution.py:102
  505.4 13.0 %fusion.1 = (f32[1536,1536]{1,0:T(8,128)}, f32[1536,1536]{1,0:T(8,128)}) fusion(f32[1536,1536]{1,0:T(8,128)} %get-tuple-element.25, pred[]{:T(512)S(6)} %cholesky.891), kind=kLoop, calls=%fused_computation.9 | loop fusion | flops 9437184 | bytes 28311552 | tf_op jit(solution)/shard_map/triangular_solve | solution.py:107
  518.4 34.8 %while.1 = (s32[]{:T(128)}, f32[1536,1536]{1,0:T(8,128)}, s32[12,2]{0,1:T(2,128)S(1)}, f32[12,128,128]{2,1,0:T(8,128)S(1)}, s32[]{:T(128)}) while((s32[]{:T(128)}, f32[1536,1536]{1,0:T(8,128)}, s32[12,2]{0,1:T(2,128)S(1)}, f32[12,128,128]{2,1,0:T(8,128)S(1)}, s32[]{:T(128)}) %tuple.108), condition=%wide.while_cond, body=%wide.while_body.sunk | while | flops 2 | bytes 131189 | solution.py:107
  553.3 117.9 %custom-call.105 = f32[12,128,128]{1,2,0:T(8,128)S(1)} custom-call(f32[12,128,128]{2,1,0:T(8,128)S(1)} %get-tuple-element.11), custom_call_target="InvertDiagBlocksLowerTriangular" | custom-call | tf_op jit(solution)/shard_map/triangular_solve | solution.py:107
  700.6 137.7 %all-gather.10.cloned.1.call-done = f32[1408,1536]{1,0:T(8,128)} async-done(((f32[88,1536]{1,0:T(8,128)}), f32[1408,1536]{1,0:T(8,128)}) %all-gather.10.cloned.1.call-update) | async-done | bytes 8650768 | tf_op jit(solution)/shard_map/all_gather | solution.py:110
  849.4 22.9 %all-to-all-done.2 = f32[1,1408,352]{1,0,2:T(1,128)S(1)} async-done(((f32[1,1408,352]{1,0,2:T(1,128)}), f32[1,1408,352]{1,0,2:T(1,128)S(1)}, u32[]{:S(2)}, u32[]{:S(2)}) %all-to-all-start.2) | async-done | bytes 1982496 | tf_op jit(solution)/shard_map/all_to_all | solution.py:87
  897.2 21.3 %all-to-all-done.3 = f32[4,1408,88]{1,2,0:T(8,128)S(1)} async-done(((f32[4,1408,88]{1,2,0:T(8,128)}), f32[4,1408,88]{1,2,0:T(8,128)S(1)}, u32[]{:S(2)}, u32[]{:S(2)}) %all-to-all-start.3) | async-done | bytes 1982496 | tf_op jit(solution)/shard_map/all_to_all | solution.py:96
  926.1 14.4 %fusion.2 = f32[1,1408,352]{1,2,0:T(8,128)} fusion(f32[1408,352]{0,1:T(8,128)S(1)} %bitcast.193, f32[1408,1536]{1,0:T(8,128)} %all-gather.10.cloned.1.call-done, f32[4,352,1536]{2,1,0:T(8,128)} %bitcast.203, s32[]{:T(128)S(6)} %select_n.67), kind=kOutput, calls=%fused_computation.11 | convolution fusion | flops 9135689728 | bytes 14778372 | tf_op jit(solution)/shard_map/dot_general | solution.py:118
  (182 shorter events, 329.5 us)
Async XLA Ops:
  10.0 15.1 %all-to-all-start = ((f32[1,112,1536]{1,0,2:T(1,128)}), f32[1,112,1536]{1,0,2:T(1,128)S(1)}, u32[]{:S(2)}, u32[]{:S(2)}) async-start(f32[1,112,1536]{1,0,2:T(1,128)} %copy.38), calls=%async_computation | async-start | bytes 1572864 | tf_op jit(solution)/shard_map/all_to_all | solution.py:31
  14.8 103.0 %all-gather.6.cloned.1.call-start = ((), (), s32[]{:S(2)}) async-start(), calls=%async_computation.5 | async-start | bytes 5308416 | tf_op jit(solution)/shard_map/all_gather | solution.py:47
  52.9 93.2 %all-gather.8.cloned.1.call-start = ((), (), s32[]{:S(2)}) async-start(), calls=%async_computation.6 | async-start | bytes 14155776 | tf_op jit(solution)/shard_map/all_gather | solution.py:47
  117.9 720.4 %all-gather.10.cloned.1.call-start = ((), (), s32[]{:S(2)}) async-start(), calls=%async_computation.7 | async-start | bytes 9191424 | tf_op jit(solution)/shard_map/all_gather | solution.py:110
  671.2 1.4 copy-start.1
  672.8 168.8 %copy-start = (f32[1,1408,352]{1,2,0:T(8,128)S(1)}, f32[1,1408,352]{1,2,0:T(8,128)}, u32[]{:S(2)}) copy-start(f32[1,1408,352]{1,2,0:T(8,128)} %param.9) | copy-start | bytes 5947396
  690.7 158.1 %copy-start.3 = (s32[2]{0:T(128)S(1)}, s32[2]{0:T(128)}, u32[]{:S(2)}) copy-start(s32[2]{0:T(128)} %param.5) | copy-start | bytes 28
  699.7 0.8 copy-start.2
  700.5 225.5 %all-gather.12.cloned.1.call-start = ((), (), s32[]{:S(2)}) async-start(), calls=%async_computation.8 | async-start | bytes 10813440 | tf_op jit(solution)/shard_map/all_gather | solution.py:59
  844.9 27.5 %all-to-all-start.2 = ((f32[1,1408,352]{1,0,2:T(1,128)}), f32[1,1408,352]{1,0,2:T(1,128)S(1)}, u32[]{:S(2)}, u32[]{:S(2)}) async-start(f32[1,1408,352]{1,0,2:T(1,128)} %copy.44), calls=%async_computation.2 | async-start | bytes 3964928 | tf_op jit(solution)/shard_map/all_to_all | solution.py:87
  873.6 17.0 %all-to-all-start.4 = ((f32[64,1,1]{2,1,0:T(1,128)}), f32[64,1,1]{2,1,0:T(1,128)S(1)}, u32[]{:S(2)}, u32[]{:S(2)}) async-start(f32[64,1,1]{2,1,0:T(1,128)} %broadcast_in_dim.56), calls=%async_computation.4 | async-start | bytes 65536 | tf_op jit(solution)/shard_map/all_to_all | solution.py:15
  890.7 27.8 %all-to-all-start.3 = ((f32[4,1408,88]{1,2,0:T(8,128)}), f32[4,1408,88]{1,2,0:T(8,128)S(1)}, u32[]{:S(2)}, u32[]{:S(2)}) async-start(f32[4,1408,88]{1,2,0:T(8,128)} %broadcast_select_fusion), calls=%async_computation.3 | async-start | bytes 3964928 | tf_op jit(solution)/shard_map/all_to_all | solution.py:96
Sparse Core Ops, SparseCore 0:
  53.1 64.7 all-gather.5
  119.7 26.4 all-gather.7
  700.7 137.5 all-gather.9
  841.7 84.3 all-gather.11
where the time goes:
time: 954 us; the launch traced here: 948 us
  other arithmetic  412 us (43%)
  waiting for transfers between devices  296 us (31%)
  matrix products  92.9 us (10%)
  local copies, waits for them, and re-layouts  76.6 us (8%)
  blocking collectives  26 us (3%)
  between operations  24 us (3%)
  starting transfers between devices  20.6 us (2%)
    another operation x46, other arithmetic, local(): factor_low = jnp.linalg.cholesky(gathered)  264 us
    all_gather x1, waiting for transfers between devices, local(): row_block = lax.all_gather(own_rows, COL, axis=0, tiled=True)  138 us
    another operation x3, other arithmetic, local(): lax.linalg.triangular_solve(factor_low, below_block, left_side=False, low...  131 us
    all_gather x2, waiting for transfers between devices, gather_in_order(): pieces = lax.all_gather(pieces, axes[k], axis=0, tiled=True)  93 us
    another operation x22, matrix products, local(): factor_low = jnp.linalg.cholesky(gathered)  50.1 us
    another operation x36, local copies, waits for them, and re-layouts  34.6 us
    another operation x23, matrix products, local(): lax.linalg.triangular_solve(factor_low, below_block, left_side=False, low...  28.4 us
    all_to_all x1, waiting for transfers between devices, local(): lax.all_to_all(trailing, 'sub', split_axis=2, concat_axis=0, tiled=True)  22.9 us
  transfers between devices with their start and end apart: 8, of which 8 were waited for; matrix products, arithmetic and copies ran while one was open for 1% of the time, Pallas kernels for 0%

commit v1 on v0

--- a/solution.py
+++ b/solution.py
@@ -8,6 +8,13 @@
 COL = ("col_0", "col_1")
 ROW_COL = ("row_0", "row_1", "col_0", "col_1")
 SUB_ROW_COL = ("sub", "row_0", "row_1", "col_0", "col_1")
+
+
+def swapped_in(value, mesh_axis, along):
+    size = lax.axis_size(mesh_axis)
+    blocks = jnp.stack([value for _ in range(size)])
+    blocks = lax.all_to_all(blocks, mesh_axis, split_axis=0, concat_axis=0)
+    return jnp.concatenate(blocks, axis=along)
 
 
 def from_everyone(value, axis):
@@ -107,7 +114,7 @@
     own_rows = lax.linalg.triangular_solve(
         factor_low, below_block, left_side=False, lower=True, transpose_a=True
     )
-    row_block = lax.all_gather(own_rows, COL, axis=0, tiled=True)
+    row_block = swapped_in(own_rows, COL, 0)
     col_block = column_rows(
         row_block,
         rows_count,

time: 954 us -> 1020 us (1.069)
  waiting for transfers between devices: 296 us -> 355 us
  starting transfers between devices: 20.6 us -> 34.1 us
    all_to_all x0 -> x1, waiting for transfers between devices: none -> 198 us  [swapped_in(): blocks = lax.all_to_all(blocks, mesh_axis, split_axis=0, concat_axis=0)]
    all_gather x1 -> x0, waiting for transfers between devices: 138 us -> none  [local(): row_block = lax.all_gather(own_rows, COL, axis=0, tiled=True)]
    another operation x36 -> x37, local copies, waits for them, and re-layouts: 34.6 us -> 39.1 us
where the time goes in v1:
time: 1020 us
  other arithmetic  412 us (40%)
  waiting for transfers between devices  355 us (35%)
  matrix products  84.4 us (8%)
  local copies, waits for them, and re-layouts  80.2 us (8%)
  starting transfers between devices  34.1 us (3%)
  blocking collectives  26 us (3%)
  between operations  24 us (2%)
    another operation x46, other arithmetic, local(): factor_low = jnp.linalg.cholesky(gathered)  264 us
    all_to_all x1, waiting for transfers between devices, swapped_in(): blocks = lax.all_to_all(blocks, mesh_axis, split_axis=0, concat_axis=0)  198 us
    another operation x3, other arithmetic, local(): lax.linalg.triangular_solve(factor_low, below_block, left_side=False, low...  131 us
    all_gather x2, waiting for transfers between devices, gather_in_order(): pieces = lax.all_gather(pieces, axes[k], axis=0, tiled=True)  93.1 us
    another operation x22, matrix products, local(): factor_low = jnp.linalg.cholesky(gathered)  50.1 us
    another operation x36, local copies, waits for them, and re-layouts  34.6 us
    all_to_all x1, waiting for transfers between devices, local(): lax.all_to_all(trailing, 'sub', split_axis=2, concat_axis=0, tiled=True)  22.9 us
    all_to_all x1, waiting for transfers between devices, local(): lax.all_to_all(ordered[2], 'sub', split_axis=0, concat_axis=2, tiled=True)  21.3 us
  transfers between devices with their start and end apart: 8, of which 8 were waited for; matrix products, arithmetic and copies ran while one was open for 1% of the time, Pallas kernels for 0%

profile of v1, /device:TPU:1, one launch (start us, length us, event | category | flops | bytes accessed | tf_op | source)
XLA Modules:
  0.0 1016.3 jit_solution(13058286583577488880)
XLA Ops:
  26.8 10.4 %all_to_all.80 = f32[4,112,384]{2,1,0:T(8,128)S(1)} all-to-all(f32[4,112,384]{2,1,0:T(8,128)S(1)} %pad_maximum_fusion.1), channel_id=1, replica_groups=mesh['sub'=4,'row_0'=2,'row_1'=2,'col_0'=8,'col_1'=2] {'sub'}, dimensions={0} | all-to-all | bytes 1376256 | tf_op jit(solution)/shard_map/all_to_all | solution.py:38
  53.0 64.9 %all-gather.5.cloned.1.call-done = f32[32,24,1536]{2,1,0:T(8,128)} async-done(((f32[4,24,1536]{2,1,0:T(8,128)}), f32[32,24,1536]{2,1,0:T(8,128)}) %all-gather.5.cloned.1.call-update) | async-done | bytes 4718608 | tf_op jit(solution)/shard_map/all_gather | solution.py:54
  117.9 28.2 %all-gather.7.cloned.1.call-done = f32[64,24,1536]{2,1,0:T(8,128)} async-done(((f32[32,24,1536]{2,1,0:T(8,128)}), f32[64,24,1536]{2,1,0:T(8,128)}) %all-gather.7.cloned.1.call-update) | async-done | bytes 9437200 | tf_op jit(solution)/shard_map/all_gather | solution.py:54
  165.1 12.3 %fusion = f32[1536,1536]{1,0:T(8,128)} fusion(f32[1536,1536]{0,1:T(8,128)} %copy.43, f32[2,2,8,2,24,1536]{5,4,3,2,1,0:T(8,128)} %copy.42), kind=kLoop, calls=%fused_computation.6 | loop fusion | flops 4718592 | bytes 28311552 | tf_op jit(solution)/shard_map/jit(cholesky)/div | solution.py:109
  178.2 11.7 %cholesky.341 = f32[128,128]{1,0:T(8,128)S(1)} custom-call(f32[128,128]{1,0:T(8,128)S(1)} %cholesky.892), custom_call_target="Cholesky" | custom-call | tf_op jit(solution)/shard_map/jit(cholesky)/cholesky | solution.py:109
  209.4 11.9 %cholesky.362 = f32[128,128]{1,0:T(8,128)S(1)} custom-call(f32[128,128]{1,0:T(8,128)S(1)} %cholesky.896), custom_call_target="Cholesky" | custom-call | tf_op jit(solution)/shard_map/jit(cholesky)/cholesky | solution.py:109
  236.1 11.7 %cholesky.385 = f32[128,128]{1,0:T(8,128)S(1)} custom-call(f32[128,128]{1,0:T(8,128)S(1)} %cholesky.901), custom_call_target="Cholesky" | custom-call | tf_op jit(solution)/shard_map/jit(cholesky)/cholesky | solution.py:109
  263.3 11.7 %cholesky.715 = f32[128,128]{1,0:T(8,128)S(1)} custom-call(f32[128,128]{1,0:T(8,128)S(1)} %cholesky.906), custom_call_target="Cholesky" | custom-call | tf_op jit(solution)/shard_map/jit(cholesky)/cholesky | solution.py:109
  290.6 12.1 %cholesky.734 = f32[128,128]{1,0:T(8,128)S(1)} custom-call(f32[128,128]{1,0:T(8,128)S(1)} %cholesky.911), custom_call_target="Cholesky" | custom-call | tf_op jit(solution)/shard_map/jit(cholesky)/cholesky | solution.py:109
  318.4 11.7 %cholesky.754 = f32[128,128]{1,0:T(8,128)S(1)} custom-call(f32[128,128]{1,0:T(8,128)S(1)} %cholesky.916), custom_call_target="Cholesky" | custom-call | tf_op jit(solution)/shard_map/jit(cholesky)/cholesky | solution.py:109
  345.8 11.7 %cholesky.774 = f32[128,128]{1,0:T(8,128)S(1)} custom-call(f32[128,128]{1,0:T(8,128)S(1)} %cholesky.921), custom_call_target="Cholesky" | custom-call | tf_op jit(solution)/shard_map/jit(cholesky)/cholesky | solution.py:109
  373.2 11.7 %cholesky.794 = f32[128,128]{1,0:T(8,128)S(1)} custom-call(f32[128,128]{1,0:T(8,128)S(1)} %cholesky.926), custom_call_target="Cholesky" | custom-call | tf_op jit(solution)/shard_map/jit(cholesky)/cholesky | solution.py:109
  400.1 12.1 %cholesky.814 = f32[128,128]{1,0:T(8,128)S(1)} custom-call(f32[128,128]{1,0:T(8,128)S(1)} %cholesky.931), custom_call_target="Cholesky" | custom-call | tf_op jit(solution)/shard_map/jit(cholesky)/cholesky | solution.py:109
  426.9 11.7 %cholesky.834 = f32[128,128]{1,0:T(8,128)S(1)} custom-call(f32[128,128]{1,0:T(8,128)S(1)} %cholesky.936), custom_call_target="Cholesky" | custom-call | tf_op jit(solution)/shard_map/jit(cholesky)/cholesky | solution.py:109
  452.8 11.9 %cholesky.854 = f32[128,128]{1,0:T(8,128)S(1)} custom-call(f32[128,128]{1,0:T(8,128)S(1)} %cholesky.941), custom_call_target="Cholesky" | custom-call | tf_op jit(solution)/shard_map/jit(cholesky)/cholesky | solution.py:109
  478.2 11.7 %cholesky.872 = f32[128,128]{1,0:T(8,128)S(1)} custom-call(f32[128,128]{1,0:T(8,128)S(1)} %convolution_subtract_fusion.4), custom_call_target="Cholesky" | custom-call | tf_op jit(solution)/shard_map/jit(cholesky)/cholesky | solution.py:109
  505.4 13.0 %fusion.1 = (f32[1536,1536]{1,0:T(8,128)}, f32[1536,1536]{1,0:T(8,128)}) fusion(f32[1536,1536]{1,0:T(8,128)} %get-tuple-element.25, pred[]{:T(512)S(6)} %cholesky.891), kind=kLoop, calls=%fused_computation.9 | loop fusion | flops 9437184 | bytes 28311552 | tf_op jit(solution)/shard_map/triangular_solve | solution.py:114
  518.4 34.8 %while.1 = (s32[]{:T(128)}, f32[1536,1536]{1,0:T(8,128)}, s32[12,2]{0,1:T(2,128)S(1)}, f32[12,128,128]{2,1,0:T(8,128)S(1)}, s32[]{:T(128)}) while((s32[]{:T(128)}, f32[1536,1536]{1,0:T(8,128)}, s32[12,2]{0,1:T(2,128)S(1)}, f32[12,128,128]{2,1,0:T(8,128)S(1)}, s32[]{:T(128)}) %tuple.108), condition=%wide.while_cond, body=%wide.while_body.sunk | while | flops 2 | bytes 131189 | solution.py:114
  553.3 117.9 %custom-call.105 = f32[12,128,128]{1,2,0:T(8,128)S(1)} custom-call(f32[12,128,128]{2,1,0:T(8,128)S(1)} %get-tuple-element.11), custom_call_target="InvertDiagBlocksLowerTriangular" | custom-call | tf_op jit(solution)/shard_map/triangular_solve | solution.py:114
  705.0 197.9 %all-to-all-done.4 = f32[16,88,1536]{2,1,0:T(8,128)} async-done(((f32[16,88,1536]{2,1,0:T(8,128)}), f32[16,88,1536]{2,1,0:T(8,128)}, u32[]{:S(2)}, u32[]{:S(2)}) %all-to-all-start.4) | async-done | bytes 8650784 | tf_op jit(solution)/shard_map/all_to_all | solution.py:16
  914.1 22.9 %all-to-all-done.2 = f32[1,1408,352]{1,0,2:T(1,128)S(1)} async-done(((f32[1,1408,352]{1,0,2:T(1,128)}), f32[1,1408,352]{1,0,2:T(1,128)S(1)}, u32[]{:S(2)}, u32[]{:S(2)}) %all-to-all-start.2) | async-done | bytes 1982496 | tf_op jit(solution)/shard_map/all_to_all | solution.py:94
  938.3 12.4 %all-to-all-start.5 = ((f32[64,1,1]{2,1,0:T(1,128)}), f32[64,1,1]{2,1,0:T(1,128)S(1)}, u32[]{:S(2)}, u32[]{:S(2)}) async-start(f32[64,1,1]{2,1,0:T(1,128)} %broadcast_in_dim.56), calls=%async_computation.5 | async-start | bytes 65536 | tf_op jit(solution)/shard_map/all_to_all | solution.py:22
  966.2 21.3 %all-to-all-done.3 = f32[4,1408,88]{1,2,0:T(8,128)S(1)} async-done(((f32[4,1408,88]{1,2,0:T(8,128)}), f32[4,1408,88]{1,2,0:T(8,128)S(1)}, u32[]{:S(2)}, u32[]{:S(2)}) %all-to-all-start.3) | async-done | bytes 1982496 | tf_op jit(solution)/shard_map/all_to_all | solution.py:103
  994.0 14.4 %fusion.2 = f32[1,1408,352]{1,2,0:T(8,128)} fusion(f32[1408,352]{0,1:T(8,128)S(1)} %bitcast.194, f32[1408,1536]{1,0:T(8,128)} %bitcast.54, f32[4,352,1536]{2,1,0:T(8,128)} %bitcast.204, s32[]{:T(128)S(6)} %select_n.67), kind=kOutput, calls=%fused_computation.11 | convolution fusion | flops 9135689728 | bytes 14778372 | tf_op jit(solution)/shard_map/dot_general | solution.py:125
  (180 shorter events, 334.9 us)
Async XLA Ops:
  10.0 15.1 %all-to-all-start = ((f32[1,112,1536]{1,0,2:T(1,128)}), f32[1,112,1536]{1,0,2:T(1,128)S(1)}, u32[]{:S(2)}, u32[]{:S(2)}) async-start(f32[1,112,1536]{1,0,2:T(1,128)} %copy.38), calls=%async_computation | async-start | bytes 1572864 | tf_op jit(solution)/shard_map/all_to_all | solution.py:38
  14.8 103.0 %all-gather.5.cloned.1.call-start = ((), (), s32[]{:S(2)}) async-start(), calls=%async_computation.6 | async-start | bytes 5308416 | tf_op jit(solution)/shard_map/all_gather | solution.py:54
  52.9 93.2 %all-gather.7.cloned.1.call-start = ((), (), s32[]{:S(2)}) async-start(), calls=%async_computation.7 | async-start | bytes 14155776 | tf_op jit(solution)/shard_map/all_gather | solution.py:54
  691.1 4.5 copy-start.1
  695.7 210.5 %copy-start = (f32[1,1408,352]{1,2,0:T(8,128)S(1)}, f32[1,1408,352]{1,2,0:T(8,128)}, u32[]{:S(2)}) copy-start(f32[1,1408,352]{1,2,0:T(8,128)} %param.9) | copy-start | bytes 5947396
  695.7 207.2 %all-to-all-start.4 = ((f32[16,88,1536]{2,1,0:T(8,128)}), f32[16,88,1536]{2,1,0:T(8,128)}, u32[]{:S(2)}, u32[]{:S(2)}) async-start(f32[16,88,1536]{2,1,0:T(8,128)} %stack.2), calls=%async_computation.4 | async-start | bytes 17301504 | tf_op jit(solution)/shard_map/all_to_all | solution.py:16
  704.9 208.6 %copy-start.2 = (s32[2]{0:T(128)S(1)}, s32[2]{0:T(128)}, u32[]{:S(2)}) copy-start(s32[2]{0:T(128)} %param.5) | copy-start | bytes 28
  704.9 289.1 %all-gather.9.cloned.1.call-start = ((), (), s32[]{:S(2)}) async-start(), calls=%async_computation.8 | async-start | bytes 10813440 | tf_op jit(solution)/shard_map/all_gather | solution.py:66
  909.5 27.6 %all-to-all-start.2 = ((f32[1,1408,352]{1,0,2:T(1,128)}), f32[1,1408,352]{1,0,2:T(1,128)S(1)}, u32[]{:S(2)}, u32[]{:S(2)}) async-start(f32[1,1408,352]{1,0,2:T(1,128)} %copy.44), calls=%async_computation.2 | async-start | bytes 3964928 | tf_op jit(solution)/shard_map/all_to_all | solution.py:94
  938.3 21.4 %all-to-all-start.5 = ((f32[64,1,1]{2,1,0:T(1,128)}), f32[64,1,1]{2,1,0:T(1,128)S(1)}, u32[]{:S(2)}, u32[]{:S(2)}) async-start(f32[64,1,1]{2,1,0:T(1,128)} %broadcast_in_dim.56), calls=%async_computation.5 | async-start | bytes 65536 | tf_op jit(solution)/shard_map/all_to_all | solution.py:22
  959.7 27.9 %all-to-all-start.3 = ((f32[4,1408,88]{1,2,0:T(8,128)}), f32[4,1408,88]{1,2,0:T(8,128)S(1)}, u32[]{:S(2)}, u32[]{:S(2)}) async-start(f32[4,1408,88]{1,2,0:T(8,128)} %broadcast_select_fusion), calls=%async_computation.3 | async-start | bytes 3964928 | tf_op jit(solution)/shard_map/all_to_all | solution.py:103
Sparse Core Ops, SparseCore 0:
  53.1 64.7 all-gather.4
  119.7 26.4 all-gather.6
  906.3 87.6 all-gather.8
